TPU v7x, 32 devices: a whole 2x2x4 slice. The times are simulated.
32 devices in a mesh: ty: 4 (over y, x), tx: 8 (over z, core).
Axes of the slice: x: 2, y: 2, z: 4, core: 2. Of those that a mesh axis runs over, the one named last changes fastest.
Arguments:
- object_slices: float32 [2, 2, 1024, 2048], P(None, None, 'ty', 'tx'), may hold values from -5 to 5
- probe: float32 [2, 256, 256], replicated, may hold values from -5 to 5
- position_count: int32 [4, 8], P('ty', 'tx'), may hold values from 1 to 5, as said below
- offsets: int32 [4, 8, 5, 2], P('ty', 'tx'), may hold values from 0 to 128
- intensities: float32 [4, 8, 5, 256, 256], P('ty', 'tx'), may hold values from 0 to 2
Outputs:
- object_new: float32 [2, 2, 1024, 2048], P(None, None, 'ty', 'tx')
- probe_new: float32 [2, 256, 256], replicated
Inputs may be any that keep to these rules, and one draw needn't show every extreme that they name: `position_count`: each tile has 1 to 5 positions; some tile has exactly 5.
All inputs are finite; a program needn't handle non-finite values.
Results may differ from a plain program's by a relative error of at most 0.0003.
Values sent between devices are 32-bit elements; how exact they have to be, the bound alone decides.
No kernel may reach another device: no remote copies, remote signals or barrier semaphores. Data moves between devices by JAX's collectives and lax.ppermute only.
A program may use at most 128 MiB of HBM per device.

v0:
```python
import math

import jax
import jax.numpy as jnp
from jax import lax
from jax.sharding import PartitionSpec as P

PROBE = 256
CORE = 256
MARGIN = 64
ITERS = 2


chirp_rate = 0.5
object_rate = 0.5
probe_rate = 2.0


def extended_2(block, sides, width):
    for axis, dim in sides:
        count = lax.axis_size(axis)
        forward = [(i, i + 1) for i in range(count - 1)]
        forward.append((count - 1, 0))
        backward = [(target, source) for source, target in forward]
        low = lax.ppermute(
            lax.slice_in_dim(block, block.shape[dim] - width, None, axis=dim), axis, forward
        )
        high = lax.ppermute(lax.slice_in_dim(block, 0, width, axis=dim), axis, backward)
        block = jnp.concatenate([low, block, high], axis=dim)
    return block


def matmul(left, right):
    return jnp.dot(left, right, precision=lax.Precision.HIGHEST, preferred_element_type=jnp.float32)


def complex_product(left_real, left_imag, right_real, right_imag):
    out_real = matmul(left_real, right_real) - matmul(left_imag, right_imag)
    out_imag = matmul(left_real, right_imag) + matmul(left_imag, right_real)
    return (out_real, out_imag)


def dft_tables(size):
    index = lax.iota(jnp.int32, size)
    product = index[:, None] * index[None, :] % size
    angles = product.astype(jnp.float32) * (2.0 * math.pi / size)
    factor = 1.0 / math.sqrt(size)
    four_real = jnp.cos(angles) * factor
    four_imag = -jnp.sin(angles) * factor
    centred = ((index + size // 2) % size - size // 2).astype(jnp.float32)
    phases = centred * centred * (chirp_rate * math.pi / size)
    kernel_real = jnp.cos(phases)
    kernel_imag = -jnp.sin(phases)
    scaled_real = four_real * kernel_real[None, :] + four_imag * kernel_imag[None, :]
    scaled_imag = four_real * kernel_imag[None, :] - four_imag * kernel_real[None, :]
    prop_real, prop_imag = complex_product(scaled_real, scaled_imag, four_real, four_imag)
    return (four_real, four_imag, prop_real, prop_imag)


def forward_pair(mat_real, mat_imag, field_real, field_imag):
    mid_real, mid_imag = complex_product(mat_real, mat_imag, field_real, field_imag)
    return complex_product(mid_real, mid_imag, mat_real.T, mat_imag.T)


def adjoint_pair(mat_real, mat_imag, field_real, field_imag):
    mid_real, mid_imag = complex_product(mat_real.T, -mat_imag.T, field_real, field_imag)
    return complex_product(mid_real, mid_imag, mat_real, -mat_imag)


def position_grad(probe_now, window, measured, tables):
    four_real, four_imag, prop_real, prop_imag = tables
    probe_real, probe_imag = (probe_now[0], probe_now[1])
    one_real, one_imag, two_real, two_imag = (window[0], window[1], window[2], window[3])
    wave_real = probe_real * one_real - probe_imag * one_imag
    wave_imag = probe_real * one_imag + probe_imag * one_real
    moved_real, moved_imag = forward_pair(prop_real, prop_imag, wave_real, wave_imag)
    exit_real = moved_real * two_real - moved_imag * two_imag
    exit_imag = moved_real * two_imag + moved_imag * two_real
    far_real, far_imag = forward_pair(four_real, four_imag, exit_real, exit_imag)
    misfit = far_real * far_real + far_imag * far_imag - measured
    back_real, back_imag = adjoint_pair(four_real, four_imag, misfit * far_real, misfit * far_imag)
    grad_two_real = moved_real * back_real + moved_imag * back_imag
    grad_two_imag = moved_real * back_imag - moved_imag * back_real
    gmove_real = two_real * back_real + two_imag * back_imag
    gmove_imag = two_real * back_imag - two_imag * back_real
    gwave_real, gwave_imag = adjoint_pair(prop_real, prop_imag, gmove_real, gmove_imag)
    grad_one_real = probe_real * gwave_real + probe_imag * gwave_imag
    grad_one_imag = probe_real * gwave_imag - probe_imag * gwave_real
    gprobe_real = one_real * gwave_real + one_imag * gwave_imag
    gprobe_imag = one_real * gwave_imag - one_imag * gwave_real
    object_part = jnp.stack([grad_one_real, grad_one_imag, grad_two_real, grad_two_imag])
    return (object_part, jnp.stack([gprobe_real, gprobe_imag]))


def fold_axis(padded, width, dim):
    extent = padded.shape[dim] - 2 * width
    middle = lax.slice_in_dim(padded, width, width + extent, axis=dim)
    before = lax.slice_in_dim(padded, 0, width, axis=dim)
    after = lax.slice_in_dim(padded, width + extent, extent + 2 * width, axis=dim)
    spec_before = [(0, 0)] * padded.ndim
    spec_before[dim] = (2 * MARGIN - width, extent - 2 * MARGIN)
    spec_after = [(0, 0)] * padded.ndim
    spec_after[dim] = (CORE, extent - CORE - width)
    return middle + jnp.pad(before, spec_before) + jnp.pad(after, spec_after)


def fold_sums(padded, width):
    return fold_axis(fold_axis(padded, width, 1), width, 2)


def body(object_slices, probe, position_count, offsets, intensities):
    tables = dft_tables(PROBE)
    extent = CORE + 2 * MARGIN
    zero = jnp.int32(0)
    count = position_count[0, 0]
    core = object_slices.reshape(4, CORE, CORE)
    extended = extended_2(core, (("ty", 1), ("tx", 2)), MARGIN)
    probe_now = probe
    devices = lax.axis_size("ty") * lax.axis_size("tx")
    for step in range(ITERS):

        def visit(slot, carry):
            local, local_probe = carry
            top = offsets[0, 0, slot, 0]
            left = offsets[0, 0, slot, 1]
            window = lax.dynamic_slice(extended, (zero, top, left), (4, PROBE, PROBE))
            object_part, probe_part = position_grad(
                probe_now, window, intensities[0, 0, slot], tables
            )
            current = lax.dynamic_slice(local, (zero, top, left), (4, PROBE, PROBE))
            local = lax.dynamic_update_slice(local, current + object_part, (zero, top, left))
            return (local, local_probe + probe_part)

        start = (
            jnp.zeros((4, extent, extent), jnp.float32),
            jnp.zeros((2, PROBE, PROBE), jnp.float32),
        )
        grads, probe_grad = lax.fori_loop(zero, count, visit, start)
        peak = jnp.max(probe_now[0] * probe_now[0] + probe_now[1] * probe_now[1]) + 1e-06
        padded = extended_2(grads, (("ty", 1), ("tx", 2)), MARGIN)
        total = fold_sums(padded, MARGIN)[:, MARGIN : MARGIN + CORE, MARGIN : MARGIN + CORE]
        core = core - object_rate / peak * total
        if step + 1 < ITERS:
            extended = extended_2(core, (("ty", 1), ("tx", 2)), MARGIN)
        summed = lax.psum(probe_grad, ("ty", "tx"))
        probe_now = probe_now - probe_rate / devices * summed
    return (core.reshape(2, 2, CORE, CORE), probe_now)


def solution(mesh):
    placed = (
        P(None, None, "ty", "tx"),
        P(),
        P("ty", "tx"),
        P("ty", "tx", None, None),
        P("ty", "tx", None, None, None),
    )
    return jax.shard_map(
        body,
        mesh=mesh,
        in_specs=placed,
        out_specs=(P(None, None, "ty", "tx"), P()),
        check_vma=False,
    )
```

profile of v0, /device:TPU:0, one launch (start us, length us, event | category | flops | bytes accessed | tf_op | source)
XLA Modules:
  0.0 1030.2 jit_solution(13837448059332774943)
XLA Ops:
  10.0 3.0 collective-permute-start
  17.1 9.8 collective-permute-done
  26.9 10.6 %collective-permute-done.1 = f32[4,64,256]{1,2,0:T(8,128)S(1)} collective-permute-done((f32[4,64,256]{1,2,0:T(8,128)}, f32[4,64,256]{1,2,0:T(8,128)S(1)}, u32[]{:S(2)}, u32[]{:S(2)}) %collective-permute-start.1) | collective-permute-done | bytes 262176 | tf_op jit(solution)/shard_map/ppermute | solution.py:28
  38.0 3.5 collective-permute-start.3
  44.5 4.6 collective-permute-done.2
  49.1 3.1 pad_maximum_fusion.2
  54.6 87.7 %while.32 = (s32[]{:T(128)}, f32[4,384,384]{2,1,0:T(8,128)}, f32[2,256,256]{2,1,0:T(8,128)}, s32[]{:T(128)}, s32[1,1,5,2]{2,3,1,0:T(2,128)S(1)}, /*index=5*/f32[...) while((s32[]{:T(128)}, f32[4,384,384]{2,1,0:T(8,128)}, ...), condition=%wide.region_2.3_spmd.clone.clone, body=%wide.region_1.2_spmd.clone.clone.sunk | while | flops 6464077824 | bytes 48234916 | solution.py:138
  125.1 11.6 %dynamic_update_slice.16 = f32[4,384,384]{2,1,0:T(8,128)} dynamic-update-slice(f32[4,384,384]{2,1,0:T(8,128)} %get-tuple-element.1014, f32[4,256,256]{2,1,0:T(8,128)S(1)} %maximum_add_fusion.8, s32[]{:T(128)} %constant.70.clone.1..sunk, s32[]{:T(128)S(6)} %select_n.366, s32[]{:T(128)S(6)} %select_n.367) | dynamic-update-slice | bytes 2097156 | tf_op jit(solution)/shard_map/while/body/dynamic_update_slice | solution.py:131
  143.5 59.1 %collective-permute-start.4 = (f32[4,64,384]{2,1,0:T(8,128)S(1)}, f32[4,64,384]{2,1,0:T(8,128)}, u32[]{:S(2)}, u32[]{:S(2)}) collective-permute-start(f32[4,64,384]{2,1,0:T(8,128)S(1)} %get-tuple-element.748), channel_id=1, source_target_pairs={{0,8},{8,16},{16,24},{24,0},{1,9},{9,17},{17,25},{25,1},{2,10},{10... | collective-permute-start | bytes 1179656 | tf_op jit(solution)/shard_map/ppermute | solution.py:25
  202.5 57.9 %collective-permute-start.5 = (f32[4,64,384]{2,1,0:T(8,128)S(1)}, f32[4,64,384]{2,1,0:T(8,128)S(1)}, u32[]{:S(2)}, u32[]{:S(2)}) collective-permute-start(f32[4,64,384]{2,1,0:T(8,128)S(1)} %get-tuple-element.749), channel_id=1, source_target_pairs={{8,0},{16,8},{24,16},{0,24},{9,1},{17,9},{25,17},{1,25},{10,2},{18... | collective-permute-start | bytes 1179656 | tf_op jit(solution)/shard_map/ppermute | solution.py:28
  260.5 3.1 copy.25
  263.5 5.1 collective-permute-done.4
  269.8 115.3 %collective-permute-done.5 = f32[4,64,384]{2,1,0:T(8,128)S(1)} collective-permute-done((f32[4,64,384]{2,1,0:T(8,128)S(1)}, f32[4,64,384]{2,1,0:T(8,128)S(1)}, u32[]{:S(2)}, u32[]{:S(2)}) %collective-permute-start.5) | collective-permute-done | bytes 393248 | tf_op jit(solution)/shard_map/ppermute | solution.py:28
  387.9 4.0 collective-permute-start.7
  393.3 5.9 collective-permute-done.6
  399.2 4.5 collective-permute-done.7
  403.8 3.0 pad_maximum_fusion
  415.6 13.3 %collective-permute-done.8 = f32[4,64,256]{1,2,0:T(8,128)S(1)} collective-permute-done((f32[4,64,256]{1,2,0:T(8,128)}, f32[4,64,256]{1,2,0:T(8,128)S(1)}, u32[]{:S(2)}, u32[]{:S(2)}) %collective-permute-start.8) | collective-permute-done | bytes 262176 | tf_op jit(solution)/shard_map/ppermute | solution.py:25
  428.9 9.2 collective-permute-done.9
  440.5 3.4 collective-permute-start.11
  443.9 104.6 %all-reduce.11.cloned.1.call-done = f32[2,256,256]{2,1,0:T(8,128)} async-done(((f32[2,256,256]{2,1,0:T(8,128)}), f32[2,256,256]{2,1,0:T(8,128)}) %all-reduce.11.cloned.1.call-update) | async-done | bytes 524304 | tf_op jit(solution)/shard_map/psum | solution.py:145
  549.7 3.3 pad_maximum_fusion.3
  555.4 87.1 %while.33 = (s32[]{:T(128)}, f32[4,384,384]{2,1,0:T(8,128)}, f32[2,256,256]{2,1,0:T(8,128)}, s32[]{:T(128)}, s32[1,1,5,2]{2,3,1,0:T(2,128)S(1)}, /*index=5*/f32[...) while((s32[]{:T(128)}, f32[4,384,384]{2,1,0:T(8,128)}, ...), condition=%wide.region_6.7_spmd.clone.clone, body=%wide.region_5.6_spmd.clone.clone.sunk | while | flops 6464077824 | bytes 48234916 | solution.py:138
  626.4 11.6 %dynamic_update_slice.17 = f32[4,384,384]{2,1,0:T(8,128)} dynamic-update-slice(f32[4,384,384]{2,1,0:T(8,128)} %get-tuple-element.1071, f32[4,256,256]{2,1,0:T(8,128)S(1)} %maximum_add_fusion.10, s32[]{:T(128)} %constant.70.clone.1..sunk.1, s32[]{:T(128)S(6)} %select_n.385, s32[]{:T(128)S(6)} %select_n.386) | dynamic-update-slice | bytes 2097156 | tf_op jit(solution)/shard_map/while/body/dynamic_update_slice | solution.py:131
  643.7 59.6 %collective-permute-start.12 = (f32[4,64,384]{2,1,0:T(8,128)S(1)}, f32[4,64,384]{2,1,0:T(8,128)S(1)}, u32[]{:S(2)}, u32[]{:S(2)}) collective-permute-start(f32[4,64,384]{2,1,0:T(8,128)S(1)} %get-tuple-element.746), channel_id=1, source_target_pairs={{0,8},{8,16},{16,24},{24,0},{1,9},{9,17},{17,25},{25,1},{2,10},{10... | collective-permute-start | bytes 1179656 | tf_op jit(solution)/shard_map/ppermute | solution.py:25
  703.4 59.4 %collective-permute-start.13 = (f32[4,64,384]{2,1,0:T(8,128)S(1)}, f32[4,64,384]{2,1,0:T(8,128)S(1)}, u32[]{:S(2)}, u32[]{:S(2)}) collective-permute-start(f32[4,64,384]{2,1,0:T(8,128)S(1)} %get-tuple-element.747), channel_id=1, source_target_pairs={{8,0},{16,8},{24,16},{0,24},{9,1},{17,9},{25,17},{1,25},{10,2},{18... | collective-permute-start | bytes 1179656 | tf_op jit(solution)/shard_map/ppermute | solution.py:28
  762.8 3.1 copy.30
  765.9 6.0 collective-permute-done.12
  772.2 116.9 %collective-permute-done.13 = f32[4,64,384]{2,1,0:T(8,128)S(1)} collective-permute-done((f32[4,64,384]{2,1,0:T(8,128)S(1)}, f32[4,64,384]{2,1,0:T(8,128)S(1)}, u32[]{:S(2)}, u32[]{:S(2)}) %collective-permute-start.13) | collective-permute-done | bytes 393248 | tf_op jit(solution)/shard_map/ppermute | solution.py:28
  891.9 3.5 collective-permute-start.15
  896.8 116.9 %all-reduce.13.cloned.1.call-done = f32[2,256,256]{2,1,0:T(8,128)} async-done(((f32[2,256,256]{2,1,0:T(8,128)}), f32[2,256,256]{2,1,0:T(8,128)}) %all-reduce.13.cloned.1.call-update) | async-done | bytes 524304 | tf_op jit(solution)/shard_map/psum | solution.py:145
  1015.6 2.9 pad_maximum_fusion.1
  (163 shorter events, 129.3 us)
Async XLA Ops:
  7.2 541.3 %all-reduce.11.cloned.1.call-start = ((), (), s32[]{:S(2)}) async-start(), calls=%async_computation | async-start | bytes 1048576 | tf_op jit(solution)/shard_map/psum | solution.py:145
  8.8 40.3 %copy-start.3 = (f32[2,2,256,256]{2,3,1,0:T(8,128)}, f32[2,2,256,256]{2,3,1,0:T(8,128)S(1)}, u32[]{:S(2)}) copy-start(f32[2,2,256,256]{2,3,1,0:T(8,128)S(1)} %copy.21) | copy-start | bytes 3145732
  10.0 16.9 %collective-permute-start = (f32[4,64,256]{1,2,0:T(8,128)}, f32[4,64,256]{1,2,0:T(8,128)S(1)}, u32[]{:S(2)}, u32[]{:S(2)}) collective-permute-start(f32[4,64,256]{1,2,0:T(8,128)} %get-tuple-element.756), channel_id=1, source_target_pairs={{0,8},{8,16},{16,24},{24,0},{1,9},{9,17},{17,25},{25,1},{2,10},{10... | collective-permute-start | bytes 786440 | tf_op jit(solution)/shard_map/ppermute | solution.py:25
  13.0 24.6 %collective-permute-start.1 = (f32[4,64,256]{1,2,0:T(8,128)}, f32[4,64,256]{1,2,0:T(8,128)S(1)}, u32[]{:S(2)}, u32[]{:S(2)}) collective-permute-start(f32[4,64,256]{1,2,0:T(8,128)} %get-tuple-element.757), channel_id=1, source_target_pairs={{8,0},{16,8},{24,16},{0,24},{9,1},{17,9},{25,17},{1,25},{10,2},{18... | collective-permute-start | bytes 786440 | tf_op jit(solution)/shard_map/ppermute | solution.py:28
  37.6 5.4 copy-start.12
  37.9 11.2 %collective-permute-start.2 = (f32[4,384,64]{1,2,0:T(8,128)S(1)}, f32[4,384,64]{1,2,0:T(8,128)S(1)}, u32[]{:S(2)}, u32[]{:S(2)}) collective-permute-start(f32[4,384,64]{1,2,0:T(8,128)S(1)} %get-tuple-element.752), channel_id=1, source_target_pairs={{0,1},{1,2},{2,3},{3,4},{4,5},{5,6},{6,7},{7,0},{8,9},{9,10},{10,1... | collective-permute-start | bytes 1179656 | tf_op jit(solution)/shard_map/ppermute | solution.py:25
  38.0 11.1 %collective-permute-start.3 = (f32[4,384,64]{1,2,0:T(8,128)S(1)}, f32[4,384,64]{1,2,0:T(8,128)S(1)}, u32[]{:S(2)}, u32[]{:S(2)}) collective-permute-start(f32[4,384,64]{1,2,0:T(8,128)S(1)} %get-tuple-element.753), channel_id=1, source_target_pairs={{1,0},{2,1},{3,2},{4,3},{5,4},{6,5},{7,6},{0,7},{9,8},{10,9},{11,1... | collective-permute-start | bytes 1179656 | tf_op jit(solution)/shard_map/ppermute | solution.py:28
  44.5 10.1 copy-start
  44.5 10.1 copy-start.13
  119.8 3.1 copy-start.9
  123.1 13.6 %copy-start.10 = (f32[2,256,256]{2,1,0:T(8,128)}, f32[2,256,256]{2,1,0:T(8,128)S(1)}, u32[]{:S(2)}) copy-start(f32[2,256,256]{2,1,0:T(8,128)S(1)} %maximum_add_fusion.9) | copy-start | bytes 1572868 | tf_op jit(solution)/shard_map/while
  143.5 125.1 %collective-permute-start.4 = (f32[4,64,384]{2,1,0:T(8,128)S(1)}, f32[4,64,384]{2,1,0:T(8,128)}, u32[]{:S(2)}, u32[]{:S(2)}) collective-permute-start(f32[4,64,384]{2,1,0:T(8,128)S(1)} %get-tuple-element.748), channel_id=1, source_target_pairs={{0,8},{8,16},{16,24},{24,0},{1,9},{9,17},{17,25},{25,1},{2,10},{10... | collective-permute-start | bytes 1179656 | tf_op jit(solution)/shard_map/ppermute | solution.py:25
  202.5 182.6 %collective-permute-start.5 = (f32[4,64,384]{2,1,0:T(8,128)S(1)}, f32[4,64,384]{2,1,0:T(8,128)S(1)}, u32[]{:S(2)}, u32[]{:S(2)}) collective-permute-start(f32[4,64,384]{2,1,0:T(8,128)S(1)} %get-tuple-element.749), channel_id=1, source_target_pairs={{8,0},{16,8},{24,16},{0,24},{9,1},{17,9},{25,17},{1,25},{10,2},{18... | collective-permute-start | bytes 1179656 | tf_op jit(solution)/shard_map/ppermute | solution.py:28
  387.9 11.3 %collective-permute-start.6 = (f32[4,512,64]{1,2,0:T(8,128)}, f32[4,512,64]{1,2,0:T(8,128)}, u32[]{:S(2)}, u32[]{:S(2)}) collective-permute-start(f32[4,512,64]{1,2,0:T(8,128)} %get-tuple-element.740), channel_id=1, source_target_pairs={{0,1},{1,2},{2,3},{3,4},{4,5},{5,6},{6,7},{7,0},{8,9},{9,10},{10,1... | collective-permute-start | bytes 1572872 | tf_op jit(solution)/shard_map/ppermute | solution.py:25
  387.9 15.8 %collective-permute-start.7 = (f32[4,512,64]{1,2,0:T(8,128)}, f32[4,512,64]{1,2,0:T(8,128)}, u32[]{:S(2)}, u32[]{:S(2)}) collective-permute-start(f32[4,512,64]{1,2,0:T(8,128)} %get-tuple-element.741), channel_id=1, source_target_pairs={{1,0},{2,1},{3,2},{4,3},{5,4},{6,5},{7,6},{0,7},{9,8},{10,9},{11,1... | collective-permute-start | bytes 1572872 | tf_op jit(solution)/shard_map/ppermute | solution.py:28
  393.3 13.5 %copy-start.2 = (f32[4,384,384]{1,2,0:T(8,128)S(1)}, f32[4,384,384]{1,2,0:T(8,128)}, u32[]{:S(2)}) copy-start(f32[4,384,384]{1,2,0:T(8,128)} %copy.25) | copy-start | bytes 7077892
  409.6 1.2 copy-start.4
  411.4 138.3 %copy-start.5 = (f32[4,256,256]{1,2,0:T(8,128)}, f32[4,256,256]{1,2,0:T(8,128)S(1)}, u32[]{:S(2)}) copy-start(f32[4,256,256]{1,2,0:T(8,128)S(1)} %fusion.249) | copy-start | bytes 3145732
  412.6 16.3 %collective-permute-start.8 = (f32[4,64,256]{1,2,0:T(8,128)}, f32[4,64,256]{1,2,0:T(8,128)S(1)}, u32[]{:S(2)}, u32[]{:S(2)}) collective-permute-start(f32[4,64,256]{1,2,0:T(8,128)} %get-tuple-element.754), channel_id=1, source_target_pairs={{0,8},{8,16},{16,24},{24,0},{1,9},{9,17},{17,25},{25,1},{2,10},{10... | collective-permute-start | bytes 786440 | tf_op jit(solution)/shard_map/ppermute | solution.py:25
  412.6 25.5 %collective-permute-start.9 = (f32[4,64,256]{1,2,0:T(8,128)}, f32[4,64,256]{1,2,0:T(8,128)}, u32[]{:S(2)}, u32[]{:S(2)}) collective-permute-start(f32[4,64,256]{1,2,0:T(8,128)} %get-tuple-element.755), channel_id=1, source_target_pairs={{8,0},{16,8},{24,16},{0,24},{9,1},{17,9},{25,17},{1,25},{10,2},{18... | collective-permute-start | bytes 786440 | tf_op jit(solution)/shard_map/ppermute | solution.py:28
  415.6 598.1 %all-reduce.13.cloned.1.call-start = ((), (), s32[]{:S(2)}) async-start(), calls=%async_computation.1 | async-start | bytes 1048576 | tf_op jit(solution)/shard_map/psum | solution.py:145
  428.9 15.0 %copy-start.11 = (f32[4,64,256]{1,2,0:T(8,128)}, f32[4,64,256]{1,2,0:T(8,128)S(1)}, u32[]{:S(2)}) copy-start(f32[4,64,256]{1,2,0:T(8,128)S(1)} %collective-permute-done.8) | copy-start | bytes 786436
  440.3 109.3 %collective-permute-start.10 = (f32[4,384,64]{1,2,0:T(8,128)}, f32[4,384,64]{1,2,0:T(8,128)S(1)}, u32[]{:S(2)}, u32[]{:S(2)}) collective-permute-start(f32[4,384,64]{1,2,0:T(8,128)} %get-tuple-element.750), channel_id=1, source_target_pairs={{0,1},{1,2},{2,3},{3,4},{4,5},{5,6},{6,7},{7,0},{8,9},{9,10},{10,1... | collective-permute-start | bytes 1179656 | tf_op jit(solution)/shard_map/ppermute | solution.py:25
  440.5 109.2 %collective-permute-start.11 = (f32[4,384,64]{1,2,0:T(8,128)}, f32[4,384,64]{1,2,0:T(8,128)}, u32[]{:S(2)}, u32[]{:S(2)}) collective-permute-start(f32[4,384,64]{1,2,0:T(8,128)} %get-tuple-element.751), channel_id=1, source_target_pairs={{1,0},{2,1},{3,2},{4,3},{5,4},{6,5},{7,6},{0,7},{9,8},{10,9},{11,1... | collective-permute-start | bytes 1179656 | tf_op jit(solution)/shard_map/ppermute | solution.py:28
  620.5 3.1 copy-start.7
  623.8 0.8 copy-start.8
  643.7 128.2 %collective-permute-start.12 = (f32[4,64,384]{2,1,0:T(8,128)S(1)}, f32[4,64,384]{2,1,0:T(8,128)S(1)}, u32[]{:S(2)}, u32[]{:S(2)}) collective-permute-start(f32[4,64,384]{2,1,0:T(8,128)S(1)} %get-tuple-element.746), channel_id=1, source_target_pairs={{0,8},{8,16},{16,24},{24,0},{1,9},{9,17},{17,25},{25,1},{2,10},{10... | collective-permute-start | bytes 1179656 | tf_op jit(solution)/shard_map/ppermute | solution.py:25
  703.4 185.8 %collective-permute-start.13 = (f32[4,64,384]{2,1,0:T(8,128)S(1)}, f32[4,64,384]{2,1,0:T(8,128)S(1)}, u32[]{:S(2)}, u32[]{:S(2)}) collective-permute-start(f32[4,64,384]{2,1,0:T(8,128)S(1)} %get-tuple-element.747), channel_id=1, source_target_pairs={{8,0},{16,8},{24,16},{0,24},{9,1},{17,9},{25,17},{1,25},{10,2},{18... | collective-permute-start | bytes 1179656 | tf_op jit(solution)/shard_map/ppermute | solution.py:28
  891.9 123.7 %collective-permute-start.14 = (f32[4,512,64]{1,2,0:T(8,128)}, f32[4,512,64]{1,2,0:T(8,128)S(1)}, u32[]{:S(2)}, u32[]{:S(2)}) collective-permute-start(f32[4,512,64]{1,2,0:T(8,128)} %get-tuple-element.738), channel_id=1, source_target_pairs={{0,1},{1,2},{2,3},{3,4},{4,5},{5,6},{6,7},{7,0},{8,9},{9,10},{10,1... | collective-permute-start | bytes 1572872 | tf_op jit(solution)/shard_map/ppermute | solution.py:25
  891.9 123.7 %collective-permute-start.15 = (f32[4,512,64]{1,2,0:T(8,128)}, f32[4,512,64]{1,2,0:T(8,128)S(1)}, u32[]{:S(2)}, u32[]{:S(2)}) collective-permute-start(f32[4,512,64]{1,2,0:T(8,128)} %get-tuple-element.739), channel_id=1, source_target_pairs={{1,0},{2,1},{3,2},{4,3},{5,4},{6,5},{7,6},{0,7},{9,8},{10,9},{11,1... | collective-permute-start | bytes 1572872 | tf_op jit(solution)/shard_map/ppermute | solution.py:28
  1015.6 3.0 copy-start.1
  1020.2 1.2 copy-start.6
Sparse Core Ops, SparseCore 0:
  415.7 132.7 all-reduce.10
  766.0 247.5 all-reduce.12
where the time goes:
time: 1040 us; the launch traced here: 1030 us
  waiting for transfers between devices  523 us (50%)
  starting transfers between devices  258 us (25%)
  matrix products  74.3 us (7%)
  loops' own time  67 us (6%)
  local copies, waits for them, and re-layouts  58.5 us (6%)
  other arithmetic  34 us (3%)
  between operations  15.9 us (2%)
    ppermute x8, waiting for transfers between devices, extended_2(): lax.ppermute(lax.slice_in_dim(block, 0, width, axis=dim), axis, backward)  257 us
    psum x2, waiting for transfers between devices, body(): summed = lax.psum(probe_grad, ('ty', 'tx'))  221 us
    ppermute x8, starting transfers between devices, extended_2(): lax.ppermute(lax.slice_in_dim(block, 0, width, axis=dim), axis, backward)  136 us
    ppermute x8, starting transfers between devices, extended_2(): lax.ppermute(lax.slice_in_dim(block, block.shape[dim] - width, None, axis...  122 us
    dot_general x68, matrix products, matmul(): jnp.dot(left, right, precision=lax.Precision.HIGHEST, preferred_element_t...  74.3 us
    another operation x2, loops' own time, body(): grads, probe_grad = lax.fori_loop(zero, count, visit, start)  67 us
    ppermute x8, waiting for transfers between devices, extended_2(): lax.ppermute(lax.slice_in_dim(block, block.shape[dim] - width, None, axis...  44.7 us
    dynamic_update_slice x2, local copies, waits for them, and re-layouts, visit(): lax.dynamic_update_slice(local, current + object_part, (zero, top, left))  23.2 us
  transfers between devices with their start and end apart: 18, of which 13 were waited for; matrix products, arithmetic and copies ran while one was open for 2% of the time, Pallas kernels for 0%

commit v1 on v0

v1 whole, which is shorter than its diff:
```python
import math

import jax
import jax.numpy as jnp
import ml_dtypes
import numpy as np
from jax import lax
from jax.experimental import pallas as pl
from jax.experimental.pallas import tpu as pltpu
from jax.sharding import PartitionSpec as P

MARGIN = 64
ITERS = 2
CHUNK = 16

chirp_rate = 0.5
object_rate = 0.5
probe_rate = 2.0


def tables(size):
    index = np.arange(size)
    four = np.exp(-2j * np.pi * (np.outer(index, index) % size) / size) / math.sqrt(size)
    centred = (index + size // 2) % size - size // 2
    kernel = np.exp(-1j * chirp_rate * np.pi * centred * centred / size)
    prop = (four.conj() * kernel[None, :]) @ four
    half = size // 2
    near, far = prop[:half, :half], prop[:half, half:]
    blocks = ((0.5 * (near + far), 0.5 * (near - far)), (four[0::2, :half], four[1::2, :half]))
    out = np.zeros((2, 2, 2, 2, size, size), ml_dtypes.bfloat16)
    for family in range(2):
        for parity in range(2):
            block = blocks[family][parity]
            left = np.block([[block.real, -block.imag], [block.imag, block.real]])
            for form, value in enumerate((left, left.T)):
                high = value.astype(np.float32).astype(ml_dtypes.bfloat16)
                low = (value - high.astype(np.float64)).astype(np.float32).astype(ml_dtypes.bfloat16)
                out[family, parity, form, 0] = high
                out[family, parity, form, 1] = low
    return out


def lane_order(size):
    out = np.zeros((size, size), ml_dtypes.bfloat16)
    half = size // 2
    for lane in range(half):
        out[2 * lane, lane] = 1
        out[2 * lane + 1, half + lane] = 1
    return np.stack([out, out.T])


def dot(left, right):
    return jnp.dot(left, right, preferred_element_type=jnp.float32)


def parts(value):
    high = value.astype(jnp.bfloat16)
    low = (value - high.astype(jnp.float32)).astype(jnp.bfloat16)
    return high, low


def thirds(value):
    first = value.astype(jnp.bfloat16)
    rest = value - first.astype(jnp.float32)
    second = rest.astype(jnp.bfloat16)
    return first, second, (rest - second.astype(jnp.float32)).astype(jnp.bfloat16)


def sort_kernel(count_ref, values_ref, order_ref, out_ref):
    out_ref[...] = jnp.zeros_like(out_ref)

    def visit(slot, carry):
        first, second, third = [dot(x, order_ref[0]) for x in thirds(values_ref[slot])]
        first, second, third = [dot(order_ref[1], x) for x in thirds((first + second) + third)]
        out_ref[slot] = (first + second) + third
        return carry

    lax.fori_loop(0, count_ref[0], visit, 0)


def grad_kernel(
    count_ref, offset_ref, core_ref, row_ref, col_ref, corner_ref, probe_ref, measured_ref, table_ref,
    gcore_ref, grow_ref, gcol_ref, gcorner_ref, gprobe_ref,
    window_ref, moved_ref, rolled_ref, high_ref, low_ref, rhigh_ref, rlow_ref, mid_ref, back_ref,
):
    size = probe_ref.shape[1]
    half = size // 2
    quarter = size // 4
    lane = lax.broadcasted_iota(jnp.int32, (CHUNK, half), 1)
    row = lax.broadcasted_iota(jnp.int32, (CHUNK, half), 0)
    for ref in (gcore_ref, grow_ref, gcol_ref, gcorner_ref, gprobe_ref):
        ref[...] = jnp.zeros_like(ref)

    def at(part, start):
        return pl.ds(part * half + start, CHUNK)

    def lanes(part):
        return pl.ds(part * half, half)

    def fold(quads):
        mixed = [[quads[0][c] + quads[1][c] for c in range(2)], [quads[0][c] - quads[1][c] for c in range(2)]]
        return [[m[0] + m[1], m[0] - m[1]] for m in mixed]

    def put_right(start, real, imag):
        for p in range(2):
            for q in range(2):
                for comp, value in ((0, real[p][q]), (1, imag[p][q])):
                    high, low = parts(value)
                    high_ref[q, at(p, start), lanes(comp)] = high
                    low_ref[q, at(p, start), lanes(comp)] = low

    def right(family, form):
        for q in range(2):
            weight, small = table_ref[family, q, form, 0], table_ref[family, q, form, 1]
            mid_ref[q] = dot(high_ref[q], weight) + dot(low_ref[q], weight) + dot(high_ref[q], small)

    def left(family, form):
        for q in range(2):
            for p in range(2):
                for start in range(0, half, CHUNK):
                    for comp in range(2):
                        high, low = parts(mid_ref[q, at(p, start), lanes(comp)])
                        rhigh_ref[p, at(comp, start), lanes(q)] = high
                        rlow_ref[p, at(comp, start), lanes(q)] = low
        for p in range(2):
            weight, small = table_ref[family, p, form, 0], table_ref[family, p, form, 1]
            back_ref[p] = dot(weight, rhigh_ref[p]) + dot(small, rhigh_ref[p]) + dot(weight, rlow_ref[p])

    def take(start, comp):
        return [[back_ref[p, at(comp, start), lanes(q)] for q in range(2)] for p in range(2)]

    def visit(slot, carry):
        top = offset_ref[slot, 0]
        lead = offset_ref[slot, 1]
        shift_row = lax.rem(top + (size - MARGIN), size)
        shift_col = lax.rem(lead + (size - MARGIN), size)
        for comp in range(2):
            rolled_ref[comp] = pltpu.roll(pltpu.roll(probe_ref[comp], shift_row, 0), shift_col, 1)
        cols = (lane + MARGIN >= lead, lane - MARGIN < lead)

        def row_mask(part, start):
            inside = row + start
            return inside + MARGIN >= top if part == 0 else inside - MARGIN < top

        def boundary(part, start):
            return (start < quarter) == (part == 0)

        for start in range(0, half, CHUNK):
            one = [[None, None], [None, None]]
            for r in range(2):
                edge = boundary(r, start)
                mask = row_mask(r, start) if edge else None
                for c in range(2):
                    values = []
                    for k in range(4):
                        own = core_ref[k, at(r, start), lanes(c)]
                        other = col_ref[k, at(r, start), :]
                        if edge:
                            own = jnp.where(mask, own, row_ref[k, pl.ds(start, CHUNK), lanes(c)])
                            other = jnp.where(mask, other, corner_ref[k, pl.ds(start, CHUNK), :])
                        value = jnp.where(cols[c], own, other)
                        window_ref[k, at(r, start), lanes(c)] = value
                        values.append(value)
                    pr, pi = rolled_ref[0, at(r, start), lanes(c)], rolled_ref[1, at(r, start), lanes(c)]
                    one[r][c] = (pr * values[0] - pi * values[1], pr * values[1] + pi * values[0])
            real = fold([[one[r][c][0] for c in range(2)] for r in range(2)])
            imag = fold([[one[r][c][1] for c in range(2)] for r in range(2)])
            put_right(start, real, imag)
        right(0, 1)
        left(0, 0)
        for start in range(0, half, CHUNK):
            moved_real = fold(take(start, 0))
            moved_imag = fold(take(start, 1))
            real = [[None, None], [None, None]]
            imag = [[None, None], [None, None]]
            for r in range(2):
                for c in range(2):
                    mr, mi = moved_real[r][c], moved_imag[r][c]
                    moved_ref[0, at(r, start), lanes(c)] = mr
                    moved_ref[1, at(r, start), lanes(c)] = mi
                    tr, ti = window_ref[2, at(r, start), lanes(c)], window_ref[3, at(r, start), lanes(c)]
                    real[r][c] = mr * tr - mi * ti
                    imag[r][c] = mr * ti + mi * tr
            put_right(start, fold(real), fold(imag))
        right(1, 1)
        left(1, 0)
        for start in range(0, half, CHUNK):
            far_real, far_imag = take(start, 0), take(start, 1)
            real = [[None, None], [None, None]]
            imag = [[None, None], [None, None]]
            for p in range(2):
                for q in range(2):
                    fr, fi = far_real[p][q], far_imag[p][q]
                    misfit = fr * fr + fi * fi - measured_ref[slot, at(p, start), lanes(q)]
                    real[p][q] = misfit * fr
                    imag[p][q] = misfit * fi
            put_right(start, real, imag)
        right(1, 0)
        left(1, 1)

        def collect(start, k, quads):
            for r in range(2):
                edge = boundary(r, start)
                side = jnp.where(cols[0], jnp.where(cols[1], 0.0, quads[r][1]), quads[r][0])
                own = [jnp.where(cols[c], quads[r][c], 0.0) for c in range(2)]
                if edge:
                    mask = row_mask(r, start)
                    for c in range(2):
                        gcore_ref[k, at(r, start), lanes(c)] += jnp.where(mask, own[c], 0.0)
                        grow_ref[k, pl.ds(start, CHUNK), lanes(c)] += jnp.where(mask, 0.0, own[c])
                    gcol_ref[k, at(r, start), :] += jnp.where(mask, side, 0.0)
                    gcorner_ref[k, pl.ds(start, CHUNK), :] += jnp.where(mask, 0.0, side)
                else:
                    for c in range(2):
                        gcore_ref[k, at(r, start), lanes(c)] += own[c]
                    gcol_ref[k, at(r, start), :] += side

        def empty():
            return [[None, None], [None, None]]

        for start in range(0, half, CHUNK):
            back_real = fold(take(start, 0))
            back_imag = fold(take(start, 1))
            real, imag, two_real, two_imag = empty(), empty(), empty(), empty()
            for r in range(2):
                for c in range(2):
                    br, bi = back_real[r][c], back_imag[r][c]
                    mr, mi = moved_ref[0, at(r, start), lanes(c)], moved_ref[1, at(r, start), lanes(c)]
                    tr, ti = window_ref[2, at(r, start), lanes(c)], window_ref[3, at(r, start), lanes(c)]
                    two_real[r][c] = mr * br + mi * bi
                    two_imag[r][c] = mr * bi - mi * br
                    real[r][c] = tr * br + ti * bi
                    imag[r][c] = tr * bi - ti * br
            collect(start, 2, two_real)
            collect(start, 3, two_imag)
            put_right(start, fold(real), fold(imag))
        right(0, 0)
        left(0, 1)
        for start in range(0, half, CHUNK):
            wave_real = fold(take(start, 0))
            wave_imag = fold(take(start, 1))
            one_real, one_imag = empty(), empty()
            for r in range(2):
                for c in range(2):
                    wr, wi = wave_real[r][c], wave_imag[r][c]
                    pr, pi = rolled_ref[0, at(r, start), lanes(c)], rolled_ref[1, at(r, start), lanes(c)]
                    fr, fi = window_ref[0, at(r, start), lanes(c)], window_ref[1, at(r, start), lanes(c)]
                    one_real[r][c] = pr * wr + pi * wi
                    one_imag[r][c] = pr * wi - pi * wr
                    moved_ref[0, at(r, start), lanes(c)] = fr * wr + fi * wi
                    moved_ref[1, at(r, start), lanes(c)] = fr * wi - fi * wr
            collect(start, 0, one_real)
            collect(start, 1, one_imag)
        back_row = lax.rem(size - shift_row, size)
        back_col = lax.rem(size - shift_col, size)
        for comp in range(2):
            gprobe_ref[comp] += pltpu.roll(pltpu.roll(moved_ref[comp], back_row, 0), back_col, 1)
        return carry

    lax.fori_loop(0, count_ref[0], visit, 0)


def sort_measured(count, values, order):
    return pl.pallas_call(
        sort_kernel,
        out_shape=jax.ShapeDtypeStruct(values.shape, values.dtype),
        in_specs=[pl.BlockSpec(memory_space=pltpu.SMEM)] + [pl.BlockSpec(memory_space=pltpu.VMEM)] * 2,
        out_specs=pl.BlockSpec(memory_space=pltpu.VMEM),
        compiler_params=pltpu.CompilerParams(vmem_limit_bytes=32 * 1024 * 1024),
        name="sort_measured",
    )(count, values, order)


def gradients(count, offsets, core, row, col, corner, probe, measured, table):
    size = probe.shape[1]
    shapes = [x.shape for x in (core, row, col, corner, probe)]
    f32, bf16 = jnp.float32, jnp.bfloat16
    return pl.pallas_call(
        grad_kernel,
        out_shape=[jax.ShapeDtypeStruct(s, f32) for s in shapes],
        in_specs=[pl.BlockSpec(memory_space=pltpu.SMEM)] * 2 + [pl.BlockSpec(memory_space=pltpu.VMEM)] * 7,
        out_specs=[pl.BlockSpec(memory_space=pltpu.VMEM)] * 5,
        scratch_shapes=[
            pltpu.VMEM((4, size, size), f32),
            pltpu.VMEM((2, size, size), f32),
            pltpu.VMEM((2, size, size), f32),
            pltpu.VMEM((2, size, size), bf16),
            pltpu.VMEM((2, size, size), bf16),
            pltpu.VMEM((2, size, size), bf16),
            pltpu.VMEM((2, size, size), bf16),
            pltpu.VMEM((2, size, size), f32),
            pltpu.VMEM((2, size, size), f32),
        ],
        compiler_params=pltpu.CompilerParams(vmem_limit_bytes=48 * 1024 * 1024),
        name="gradients",
    )(count, offsets, core, row, col, corner, probe, measured, table)


def shifted(value, axis, step):
    count = lax.axis_size(axis)
    return lax.ppermute(value, axis, [(i, (i + step) % count) for i in range(count)])


def pack(value):
    rows = value.shape[1] // 2
    return jnp.concatenate([value[:, :rows], value[:, rows:]], axis=2)


def unpack(from_right, from_left):
    parts_of = [
        jnp.concatenate([from_right[..., s], from_left[..., s]], axis=2)
        for s in (slice(0, MARGIN), slice(MARGIN, None))
    ]
    return jnp.concatenate(parts_of, axis=1)


def swap_cols(to_left, to_right):
    return unpack(shifted(pack(to_left), "tx", -1), shifted(pack(to_right), "tx", 1))


def surroundings(core):
    size = core.shape[1]
    from_below = shifted(core[:, :MARGIN], "ty", -1)
    from_above = shifted(core[:, size - MARGIN :], "ty", 1)
    col = swap_cols(core[:, :, :MARGIN], core[:, :, size - MARGIN :])
    row = jnp.concatenate([from_below, from_above], axis=1)
    corner = swap_cols(row[:, :, :MARGIN], row[:, :, size - MARGIN :])
    return row, col, corner


def spread_cols(side, size):
    gap = jnp.zeros(side.shape[:2] + (size - 2 * MARGIN,), side.dtype)
    return jnp.concatenate([side[:, :, :MARGIN], gap, side[:, :, MARGIN:]], axis=2)


def gather_sums(gcore, grow, gcol, gcorner):
    size = gcore.shape[1]

    def to_owner(side):
        from_left = shifted(pack(side[:, :, :MARGIN]), "tx", 1)
        from_right = shifted(pack(side[:, :, MARGIN:]), "tx", -1)
        return spread_cols(unpack(from_left, from_right), size)

    grow = grow + to_owner(gcorner)
    from_above = shifted(grow[:, :MARGIN], "ty", 1)
    from_below = shifted(grow[:, MARGIN:], "ty", -1)
    total = gcore + to_owner(gcol)
    gap = jnp.zeros((gcore.shape[0], size - 2 * MARGIN, size), gcore.dtype)
    return total + jnp.concatenate([from_above, gap, from_below], axis=1)


def rounds(ty, tx):
    def split(axis, count, first):
        found, inner = [], 1
        while inner < count:
            members = first if inner == 1 and first else 4
            while (count // inner) % members:
                members //= 2
            if members < 2:
                members = count // inner
            found.append((axis, inner, members))
            inner *= members
        return found

    across = split("tx", tx, 2)
    return across[:1] + split("ty", ty, 0) + across[1:]


def ring(axis, inner, members, step):
    count = lax.axis_size(axis)
    pairs = []
    for i in range(count):
        low, mid, high = i % inner, (i // inner) % members, i // (inner * members)
        pairs.append((i, (high * members + (mid + step) % members) * inner + low))
    return pairs


def place(axis, inner, members):
    return (lax.axis_index(axis) // inner) % members


def scatter_round(value, axis, inner, members):
    pieces = value.reshape((members, value.shape[0] // members) + value.shape[1:])
    me = place(axis, inner, members)
    pick = lambda step: lax.dynamic_index_in_dim(pieces, (me + step) % members, 0, keepdims=False)
    out = pick(0)
    for got in [lax.ppermute(pick(s), axis, ring(axis, inner, members, s)) for s in range(1, members)]:
        out = out + got
    return out


def gather_round(value, axis, inner, members):
    me = place(axis, inner, members)
    got = [value] + [lax.ppermute(value, axis, ring(axis, inner, members, s)) for s in range(1, members)]
    out = jnp.zeros((members,) + value.shape, value.dtype)
    for step, piece in enumerate(got):
        out = lax.dynamic_update_index_in_dim(out, piece, (me + members - step) % members, 0)
    return out.reshape((members * value.shape[0],) + value.shape[1:])


def total_over_devices(value):
    flat = value.reshape(value.shape[0] * value.shape[1], value.shape[2])
    steps = rounds(lax.axis_size("ty"), lax.axis_size("tx"))
    for step in steps:
        flat = scatter_round(flat, *step)
    for step in reversed(steps):
        flat = gather_round(flat, *step)
    return flat.reshape(value.shape)


def make_body(table, order):
    def body(object_slices, probe, position_count, offsets, intensities):
        size = probe.shape[1]
        devices = lax.axis_size("ty") * lax.axis_size("tx")
        count = position_count.reshape(1)
        place_of = offsets.reshape(offsets.shape[2:])
        core = object_slices.reshape((4,) + object_slices.shape[2:])
        around = surroundings(core)
        measured = sort_measured(count, intensities.reshape(intensities.shape[2:]), order)
        for step in range(ITERS):
            *grads, gprobe = gradients(count, place_of, core, *around, probe, measured, table)
            peak = jnp.max(probe[0] * probe[0] + probe[1] * probe[1]) + 1e-06
            core = core - object_rate / peak * gather_sums(*grads)
            if step + 1 < ITERS:
                around = surroundings(core)
            probe = probe - probe_rate / devices * total_over_devices(gprobe)
        return core.reshape(object_slices.shape), probe

    return body


def solution(mesh):
    size = 256
    table, order = tables(size), lane_order(size)

    def run(object_slices, probe, position_count, offsets, intensities):
        placed = (
            P(None, None, "ty", "tx"),
            P(),
            P("ty", "tx"),
            P("ty", "tx", None, None),
            P("ty", "tx", None, None, None),
        )
        return jax.shard_map(
            make_body(jnp.asarray(table), jnp.asarray(order)),
            mesh=mesh,
            in_specs=placed,
            out_specs=(P(None, None, "ty", "tx"), P()),
            check_vma=False,
        )(object_slices, probe, position_count, offsets, intensities)

    return run
```

time: 1040 us -> 181 us (0.17); the launches traced: 1030 us -> 183 us
  waiting for transfers between devices: 523 us -> 47.1 us
  starting transfers between devices: 258 us -> 82.9 us
  matrix products: 74.3 us -> 0 us
  loops' own time: 67 us -> 0 us
  local copies, waits for them, and re-layouts: 58.5 us -> 7.82 us
  Pallas kernels: 0 us -> 32.4 us
  other arithmetic: 34 us -> 9.03 us
  between operations: 15.9 us -> 3.45 us
    ppermute x16 -> x52, waiting for transfers between devices: 301 us -> 47.1 us  [the longest x14 20.1 us: scatter_round(): lax.ppermute(pick(s), axis, ring(axis, inner, members, s))]
    psum x2 -> x0, waiting for transfers between devices: 221 us -> none  [body(): summed = lax.psum(probe_grad, ('ty', 'tx'))]
    ppermute x16 -> x52, starting transfers between devices: 258 us -> 82.9 us  [the longest x24 46.4 us: shifted(): lax.ppermute(value, axis, [(i, (i + step) % count) for i in range(count)])]
    dot_general x68 -> x0, matrix products: 74.3 us -> none  [matmul(): jnp.dot(left, right, precision=lax.Precision.HIGHEST, preferred_element_t...]
    another operation x2 -> x0, loops' own time: 67 us -> none  [body(): grads, probe_grad = lax.fori_loop(zero, count, visit, start)]
    pallas_call x0 -> x3, Pallas kernels: none -> 32.4 us  [the longest x2 30.3 us: gradients(): pl.pallas_call(grad_kernel, out_shape=[jax.ShapeDtypeStruct(s, f32) for s...]
    dynamic_update_slice x2 -> x18, local copies, waits for them, and re-layouts: 23.2 us -> 0.18 us  [gather_round(): lax.dynamic_update_index_in_dim(out, piece, (me + members - step) % membe...]
    while x18 -> x0, local copies, waits for them, and re-layouts: 11.7 us -> none  [the longest x2 6.12 us: body(): grads, probe_grad = lax.fori_loop(zero, count, visit, start)]
  transfers between devices with their start and end apart: 18 -> 52, of which waited for: 13 -> 27; matrix products, arithmetic and copies ran while one was open for 2% -> 7% of each run, Pallas kernels for 0% -> 1%
where the time goes in v1:
time: 181 us; the launch traced here: 183 us
  starting transfers between devices  82.9 us (46%)
  waiting for transfers between devices  47.1 us (26%)
  Pallas kernels  32.4 us (18%)
  other arithmetic  9.03 us (5%)
  local copies, waits for them, and re-layouts  7.82 us (4%)
  between operations  3.45 us (2%)
    ppermute x24, starting transfers between devices, shifted(): lax.ppermute(value, axis, [(i, (i + step) % count) for i in range(count)])  46.4 us
    pallas_call x2, Pallas kernels, gradients(): pl.pallas_call(grad_kernel, out_shape=[jax.ShapeDtypeStruct(s, f32) for s...  30.3 us
    ppermute x14, waiting for transfers between devices, scatter_round(): lax.ppermute(pick(s), axis, ring(axis, inner, members, s))  20.1 us
    ppermute x14, starting transfers between devices, scatter_round(): lax.ppermute(pick(s), axis, ring(axis, inner, members, s))  19.4 us
    ppermute x24, waiting for transfers between devices, shifted(): lax.ppermute(value, axis, [(i, (i + step) % count) for i in range(count)])  18.5 us
    ppermute x14, starting transfers between devices, gather_round(): lax.ppermute(value, axis, ring(axis, inner, members, s))  17.1 us
    ppermute x14, waiting for transfers between devices, gather_round(): lax.ppermute(value, axis, ring(axis, inner, members, s))  8.53 us
  transfers between devices with their start and end apart: 52, of which 27 were waited for; matrix products, arithmetic and copies ran while one was open for 7% of the time, Pallas kernels for 1%

profile of v1, /device:TPU:0, one launch (start us, length us, event | category | flops | bytes accessed | tf_op | source)
XLA Modules:
  0.0 182.6 jit_solution(12470531181883190900)
XLA Ops:
  0.6 1.9 %fusion.21 = (f32[4,64,256]{2,1,0:T(8,128)}, f32[4,64,256]{2,1,0:T(8,128)}) fusion(f32[4,256,256]{2,1,0:T(8,128)} %bitcast.119), kind=kLoop, calls=%fused_computation.94 | loop fusion | bytes 1048576 | tf_op jit(solution)/shard_map/slice | solution.py:323
  2.6 3.9 %collective-permute-start = (f32[4,64,256]{2,1,0:T(8,128)}, f32[4,64,256]{2,1,0:T(8,128)S(1)}, u32[]{:S(2)}, u32[]{:S(2)}) collective-permute-start(f32[4,64,256]{2,1,0:T(8,128)} %get-tuple-element.36), channel_id=1, source_target_pairs={{0,24},{8,0},{16,8},{24,16},{1,25},{9,1},{17,9},{25,17},{2,26},{10... | collective-permute-start | bytes 786440 | tf_op jit(solution)/shard_map/ppermute | solution.py:301
  6.9 2.8 %collective-permute-start.2 = (f32[4,128,128]{2,1,0:T(8,128)S(1)}, f32[4,128,128]{2,1,0:T(8,128)S(1)}, u32[]{:S(2)}, u32[]{:S(2)}) collective-permute-start(f32[4,128,128]{2,1,0:T(8,128)S(1)} %pad_maximum_fusion.2), channel_id=1, source_target_pairs={{0,7},{1,0},{2,1},{3,2},{4,3},{5,4},{6,5},{7,6},{8,15},{9,8},{10,9... | collective-permute-start | bytes 786440 | tf_op jit(solution)/shard_map/ppermute | solution.py:301
  14.0 2.1 %sort_measured.1.measured_ref = f32[5,256,256]{2,1,0:T(8,128)S(1)} custom-call(s32[1]{0:T(128)} %bitcast.116.count_ref, f32[5,256,256]{2,1,0:T(8,128)S(1)} %bitcast.122, bf16[2,256,256]{2,1,0:T(8,128)(2,1)S(1)} %copy-done.4), custom_call_target="tpu_custom_call" | custom-call | tf_op jit(solution)/shard_map/sort_measured/pallas_call | solution.py:264
  16.2 2.7 %collective-permute-done.1 = f32[4,64,256]{2,1,0:T(8,128)S(1)} collective-permute-done((f32[4,64,256]{2,1,0:T(8,128)}, f32[4,64,256]{2,1,0:T(8,128)S(1)}, u32[]{:S(2)}, u32[]{:S(2)}) %collective-permute-start.1) | collective-permute-done | bytes 262176 | tf_op jit(solution)/shard_map/ppermute | solution.py:301
  19.1 2.3 %collective-permute-start.4 = (f32[4,64,128]{2,1,0:T(8,128)S(1)}, f32[4,64,128]{2,1,0:T(8,128)S(1)}, u32[]{:S(2)}, u32[]{:S(2)}) collective-permute-start(f32[4,64,128]{2,1,0:T(8,128)S(1)} %pad_maximum_fusion.10), channel_id=1, source_target_pairs={{0,7},{1,0},{2,1},{3,2},{4,3},{5,4},{6,5},{7,6},{8,15},{9,8},{10,9... | collective-permute-start | bytes 393224 | tf_op jit(solution)/shard_map/ppermute | solution.py:301
  22.1 2.2 %collective-permute-done.4 = f32[4,64,128]{2,1,0:T(8,128)S(1)} collective-permute-done((f32[4,64,128]{2,1,0:T(8,128)S(1)}, f32[4,64,128]{2,1,0:T(8,128)S(1)}, u32[]{:S(2)}, u32[]{:S(2)}) %collective-permute-start.4) | collective-permute-done | bytes 131104 | tf_op jit(solution)/shard_map/ppermute | solution.py:301
  24.4 3.4 %collective-permute-done.5 = f32[4,64,128]{2,1,0:T(8,128)S(1)} collective-permute-done((f32[4,64,128]{2,1,0:T(8,128)S(1)}, f32[4,64,128]{2,1,0:T(8,128)S(1)}, u32[]{:S(2)}, u32[]{:S(2)}) %collective-permute-start.5) | collective-permute-done | bytes 131104 | tf_op jit(solution)/shard_map/ppermute | solution.py:301
  28.0 15.2 %gradients.2 = (f32[4,256,256]{2,1,0:T(8,128)S(1)}, f32[4,128,256]{2,1,0:T(8,128)S(1)}, f32[4,256,128]{2,1,0:T(8,128)S(1)}, f32[4,128,128]{2,1,0:T(8,128)S(1)}, f32[2,256,256]{2,1,0:T(8,128)S(1)}) custom-call(s32[1]{0:T(128)} %bitcast.117.count_ref, s32[5,2]{1,0:T(8,128)S(1)} %copy.9.offset_ref, f32[4,256,256]{2,1,0:T(8,128)S(1)} %bitcast.121, ...), custom_call_target="tpu_custom_call" | custom-call | tf_op jit(solution)/shard_map/gradients/pallas_call | solution.py:278
  44.2 8.6 %collective-permute-start.9 = (f32[4,64,128]{2,1,0:T(8,128)S(1)}, f32[4,64,128]{2,1,0:T(8,128)S(1)}, u32[]{:S(2)}, u32[]{:S(2)}) collective-permute-start(f32[4,64,128]{2,1,0:T(8,128)S(1)} %pad_maximum_fusion.13), channel_id=1, source_target_pairs={{0,7},{1,0},{2,1},{3,2},{4,3},{5,4},{6,5},{7,6},{8,15},{9,8},{10,9... | collective-permute-start | bytes 393224 | tf_op jit(solution)/shard_map/ppermute | solution.py:301
  53.4 3.6 %collective-permute-start.7 = (f32[4,128,128]{2,1,0:T(8,128)S(1)}, f32[4,128,128]{2,1,0:T(8,128)S(1)}, u32[]{:S(2)}, u32[]{:S(2)}) collective-permute-start(f32[4,128,128]{2,1,0:T(8,128)S(1)} %pad_maximum_fusion.5), channel_id=1, source_target_pairs={{0,7},{1,0},{2,1},{3,2},{4,3},{5,4},{6,5},{7,6},{8,15},{9,8},{10,9... | collective-permute-start | bytes 786440 | tf_op jit(solution)/shard_map/ppermute | solution.py:301
  57.6 4.9 %collective-permute-start.10 = (f32[4,64,256]{2,1,0:T(8,128)S(1)}, f32[4,64,256]{2,1,0:T(8,128)S(1)}, u32[]{:S(2)}, u32[]{:S(2)}) collective-permute-start(f32[4,64,256]{2,1,0:T(8,128)S(1)} %get-tuple-element.46), channel_id=1, source_target_pairs={{0,8},{8,16},{16,24},{24,0},{1,9},{9,17},{17,25},{25,1},{2,10},{10... | collective-permute-start | bytes 786440 | tf_op jit(solution)/shard_map/ppermute | solution.py:301
  62.6 2.1 %collective-permute-start.13 = (f32[64,256]{1,0:T(8,128)S(1)}, f32[64,256]{1,0:T(8,128)S(1)}, u32[]{:S(2)}, u32[]{:S(2)}) collective-permute-start(f32[64,256]{1,0:T(8,128)S(1)} %get-tuple-element.67), channel_id=1, source_target_pairs={{0,8},{8,16},{16,24},{24,0},{1,9},{9,17},{17,25},{25,1},{2,10},{10... | collective-permute-start | bytes 196616 | tf_op jit(solution)/shard_map/ppermute | solution.py:387
  64.8 3.3 %collective-permute-start.15 = (f32[64,256]{1,0:T(8,128)S(1)}, f32[64,256]{1,0:T(8,128)S(1)}, u32[]{:S(2)}, u32[]{:S(2)}) collective-permute-start(f32[64,256]{1,0:T(8,128)S(1)} %get-tuple-element.68), channel_id=1, source_target_pairs={{0,24},{8,0},{16,8},{24,16},{1,25},{9,1},{17,9},{25,17},{2,26},{10... | collective-permute-start | bytes 196616 | tf_op jit(solution)/shard_map/ppermute | solution.py:387
  68.2 5.6 %collective-permute-done.13 = f32[64,256]{1,0:T(8,128)S(1)} collective-permute-done((f32[64,256]{1,0:T(8,128)S(1)}, f32[64,256]{1,0:T(8,128)S(1)}, u32[]{:S(2)}, u32[]{:S(2)}) %collective-permute-start.13) | collective-permute-done | bytes 65568 | tf_op jit(solution)/shard_map/ppermute | solution.py:387
  73.8 2.1 %collective-permute-done.15 = f32[64,256]{1,0:T(8,128)S(1)} collective-permute-done((f32[64,256]{1,0:T(8,128)S(1)}, f32[64,256]{1,0:T(8,128)S(1)}, u32[]{:S(2)}, u32[]{:S(2)}) %collective-permute-start.15) | collective-permute-done | bytes 65568 | tf_op jit(solution)/shard_map/ppermute | solution.py:387
  76.1 3.7 %collective-permute-start.18 = (f32[16,256]{1,0:T(8,128)S(1)}, f32[16,256]{1,0:T(8,128)S(1)}, u32[]{:S(2)}, u32[]{:S(2)}) collective-permute-start(f32[16,256]{1,0:T(8,128)S(1)} %get-tuple-element.116), channel_id=1, source_target_pairs={{0,6},{1,7},{2,0},{3,1},{4,2},{5,3},{6,4},{7,5},{8,14},{9,15},{10,... | collective-permute-start | bytes 49160 | tf_op jit(solution)/shard_map/ppermute | solution.py:387
  82.1 2.3 %collective-permute-start.19 = (f32[16,256]{1,0:T(8,128)S(1)}, f32[16,256]{1,0:T(8,128)S(1)}, u32[]{:S(2)}, u32[]{:S(2)}) collective-permute-start(f32[16,256]{1,0:T(8,128)S(1)} %get-tuple-element.25), channel_id=1, source_target_pairs={{0,2},{1,3},{2,4},{3,5},{4,6},{5,7},{6,0},{7,1},{8,10},{9,11},{10,... | collective-permute-start | bytes 49160 | tf_op jit(solution)/shard_map/ppermute | solution.py:394
  90.4 2.2 %collective-permute-start.23 = (f32[64,256]{1,0:T(8,128)S(1)}, f32[64,256]{1,0:T(8,128)S(1)}, u32[]{:S(2)}, u32[]{:S(2)}) collective-permute-start(f32[64,256]{1,0:T(8,128)S(1)} %bitcast.141), channel_id=1, source_target_pairs={{0,16},{8,24},{16,0},{24,8},{1,17},{9,25},{17,1},{25,9},{2,18},{10... | collective-permute-start | bytes 196616 | tf_op jit(solution)/shard_map/ppermute | solution.py:394
  97.7 3.0 %collective-permute-done.26 = f32[4,64,256]{2,1,0:T(8,128)S(1)} collective-permute-done((f32[4,64,256]{2,1,0:T(8,128)S(1)}, f32[4,64,256]{2,1,0:T(8,128)S(1)}, u32[]{:S(2)}, u32[]{:S(2)}) %collective-permute-start.26) | collective-permute-done | bytes 262176 | tf_op jit(solution)/shard_map/ppermute | solution.py:301
  100.8 3.4 %collective-permute-done.27 = f32[4,64,256]{2,1,0:T(8,128)S(1)} collective-permute-done((f32[4,64,256]{2,1,0:T(8,128)S(1)}, f32[4,64,256]{2,1,0:T(8,128)S(1)}, u32[]{:S(2)}, u32[]{:S(2)}) %collective-permute-start.27) | collective-permute-done | bytes 262176 | tf_op jit(solution)/shard_map/ppermute | solution.py:301
  108.3 3.4 %collective-permute-done.31 = f32[4,64,128]{2,1,0:T(8,128)S(1)} collective-permute-done((f32[4,64,128]{2,1,0:T(8,128)}, f32[4,64,128]{2,1,0:T(8,128)S(1)}, u32[]{:S(2)}, u32[]{:S(2)}) %collective-permute-start.31) | collective-permute-done | bytes 131104 | tf_op jit(solution)/shard_map/ppermute | solution.py:301
  111.9 15.1 %gradients.3 = (f32[4,256,256]{2,1,0:T(8,128)S(1)}, f32[4,128,256]{2,1,0:T(8,128)S(1)}, f32[4,256,128]{2,1,0:T(8,128)S(1)}, f32[4,128,128]{2,1,0:T(8,128)S(1)}, f32[2,256,256]{2,1,0:T(8,128)S(1)}) custom-call(s32[1]{0:T(128)} %bitcast.118.count_ref, s32[5,2]{1,0:T(8,128)S(1)} %copy.9.offset_ref, f32[4,256,256]{2,1,0:T(8,128)S(1)} %fusion.2.core_ref, ...), custom_call_target="tpu_custom_call" | custom-call | tf_op jit(solution)/shard_map/gradients/pallas_call | solution.py:278
  128.0 7.6 %collective-permute-start.35 = (f32[4,64,128]{2,1,0:T(8,128)S(1)}, f32[4,64,128]{2,1,0:T(8,128)S(1)}, u32[]{:S(2)}, u32[]{:S(2)}) collective-permute-start(f32[4,64,128]{2,1,0:T(8,128)S(1)} %pad_maximum_fusion.17), channel_id=1, source_target_pairs={{0,7},{1,0},{2,1},{3,2},{4,3},{5,4},{6,5},{7,6},{8,15},{9,8},{10,9... | collective-permute-start | bytes 393224 | tf_op jit(solution)/shard_map/ppermute | solution.py:301
  136.2 3.6 %collective-permute-start.33 = (f32[4,128,128]{2,1,0:T(8,128)S(1)}, f32[4,128,128]{2,1,0:T(8,128)S(1)}, u32[]{:S(2)}, u32[]{:S(2)}) collective-permute-start(f32[4,128,128]{2,1,0:T(8,128)S(1)} %pad_maximum_fusion.9), channel_id=1, source_target_pairs={{0,7},{1,0},{2,1},{3,2},{4,3},{5,4},{6,5},{7,6},{8,15},{9,8},{10,9... | collective-permute-start | bytes 786440 | tf_op jit(solution)/shard_map/ppermute | solution.py:301
  140.5 4.7 %collective-permute-start.36 = (f32[4,64,256]{2,1,0:T(8,128)S(1)}, f32[4,64,256]{2,1,0:T(8,128)S(1)}, u32[]{:S(2)}, u32[]{:S(2)}) collective-permute-start(f32[4,64,256]{2,1,0:T(8,128)S(1)} %get-tuple-element.38), channel_id=1, source_target_pairs={{0,8},{8,16},{16,24},{24,0},{1,9},{9,17},{17,25},{25,1},{2,10},{10... | collective-permute-start | bytes 786440 | tf_op jit(solution)/shard_map/ppermute | solution.py:301
  145.2 2.1 %collective-permute-start.39 = (f32[64,256]{1,0:T(8,128)S(1)}, f32[64,256]{1,0:T(8,128)S(1)}, u32[]{:S(2)}, u32[]{:S(2)}) collective-permute-start(f32[64,256]{1,0:T(8,128)S(1)} %get-tuple-element.54), channel_id=1, source_target_pairs={{0,8},{8,16},{16,24},{24,0},{1,9},{9,17},{17,25},{25,1},{2,10},{10... | collective-permute-start | bytes 196616 | tf_op jit(solution)/shard_map/ppermute | solution.py:387
  148.9 2.6 %collective-permute-start.41 = (f32[64,256]{1,0:T(8,128)S(1)}, f32[64,256]{1,0:T(8,128)S(1)}, u32[]{:S(2)}, u32[]{:S(2)}) collective-permute-start(f32[64,256]{1,0:T(8,128)S(1)} %get-tuple-element.55), channel_id=1, source_target_pairs={{0,24},{8,0},{16,8},{24,16},{1,25},{9,1},{17,9},{25,17},{2,26},{10... | collective-permute-start | bytes 196616 | tf_op jit(solution)/shard_map/ppermute | solution.py:387
  151.7 5.4 %collective-permute-done.39 = f32[64,256]{1,0:T(8,128)S(1)} collective-permute-done((f32[64,256]{1,0:T(8,128)S(1)}, f32[64,256]{1,0:T(8,128)S(1)}, u32[]{:S(2)}, u32[]{:S(2)}) %collective-permute-start.39) | collective-permute-done | bytes 65568 | tf_op jit(solution)/shard_map/ppermute | solution.py:387
  157.1 2.8 %collective-permute-done.41 = f32[64,256]{1,0:T(8,128)S(1)} collective-permute-done((f32[64,256]{1,0:T(8,128)S(1)}, f32[64,256]{1,0:T(8,128)S(1)}, u32[]{:S(2)}, u32[]{:S(2)}) %collective-permute-start.41) | collective-permute-done | bytes 65568 | tf_op jit(solution)/shard_map/ppermute | solution.py:387
  160.1 3.7 %collective-permute-start.44 = (f32[16,256]{1,0:T(8,128)S(1)}, f32[16,256]{1,0:T(8,128)S(1)}, u32[]{:S(2)}, u32[]{:S(2)}) collective-permute-start(f32[16,256]{1,0:T(8,128)S(1)} %get-tuple-element.113), channel_id=1, source_target_pairs={{0,6},{1,7},{2,0},{3,1},{4,2},{5,3},{6,4},{7,5},{8,14},{9,15},{10,... | collective-permute-start | bytes 49160 | tf_op jit(solution)/shard_map/ppermute | solution.py:387
  166.2 2.3 %collective-permute-start.45 = (f32[16,256]{1,0:T(8,128)S(1)}, f32[16,256]{1,0:T(8,128)S(1)}, u32[]{:S(2)}, u32[]{:S(2)}) collective-permute-start(f32[16,256]{1,0:T(8,128)S(1)} %get-tuple-element.23), channel_id=1, source_target_pairs={{0,2},{1,3},{2,4},{3,5},{4,6},{5,7},{6,0},{7,1},{8,10},{9,11},{10,... | collective-permute-start | bytes 49160 | tf_op jit(solution)/shard_map/ppermute | solution.py:394
  (194 shorter events, 44.6 us)
Async XLA Ops:
  2.6 13.5 %collective-permute-start = (f32[4,64,256]{2,1,0:T(8,128)}, f32[4,64,256]{2,1,0:T(8,128)S(1)}, u32[]{:S(2)}, u32[]{:S(2)}) collective-permute-start(f32[4,64,256]{2,1,0:T(8,128)} %get-tuple-element.36), channel_id=1, source_target_pairs={{0,24},{8,0},{16,8},{24,16},{1,25},{9,1},{17,9},{25,17},{2,26},{10... | collective-permute-start | bytes 786440 | tf_op jit(solution)/shard_map/ppermute | solution.py:301
  6.5 12.4 %collective-permute-start.1 = (f32[4,64,256]{2,1,0:T(8,128)}, f32[4,64,256]{2,1,0:T(8,128)S(1)}, u32[]{:S(2)}, u32[]{:S(2)}) collective-permute-start(f32[4,64,256]{2,1,0:T(8,128)} %get-tuple-element.37), channel_id=1, source_target_pairs={{0,8},{8,16},{16,24},{24,0},{1,9},{9,17},{17,25},{25,1},{2,10},{10... | collective-permute-start | bytes 786440 | tf_op jit(solution)/shard_map/ppermute | solution.py:301
  6.9 14.7 %collective-permute-start.2 = (f32[4,128,128]{2,1,0:T(8,128)S(1)}, f32[4,128,128]{2,1,0:T(8,128)S(1)}, u32[]{:S(2)}, u32[]{:S(2)}) collective-permute-start(f32[4,128,128]{2,1,0:T(8,128)S(1)} %pad_maximum_fusion.2), channel_id=1, source_target_pairs={{0,7},{1,0},{2,1},{3,2},{4,3},{5,4},{6,5},{7,6},{8,15},{9,8},{10,9... | collective-permute-start | bytes 786440 | tf_op jit(solution)/shard_map/ppermute | solution.py:301
  10.6 11.2 %collective-permute-start.3 = (f32[4,128,128]{2,1,0:T(8,128)}, f32[4,128,128]{2,1,0:T(8,128)S(1)}, u32[]{:S(2)}, u32[]{:S(2)}) collective-permute-start(f32[4,128,128]{2,1,0:T(8,128)} %pad_maximum_fusion.3), channel_id=1, source_target_pairs={{0,1},{1,2},{2,3},{3,4},{4,5},{5,6},{6,7},{7,0},{8,9},{9,10},{10,1... | collective-permute-start | bytes 786440 | tf_op jit(solution)/shard_map/ppermute | solution.py:301
  43.2 19.3 %collective-permute-start.12 = (f32[256,256]{1,0:T(8,128)S(1)}, f32[256,256]{1,0:T(8,128)S(1)}, u32[]{:S(2)}, u32[]{:S(2)}) collective-permute-start(f32[256,256]{1,0:T(8,128)S(1)} %dynamic-slice_bitcast_fusion.1), channel_id=1, source_target_pairs={{0,1},{1,0},{2,3},{3,2},{4,5},{5,4},{6,7},{7,6},{8,9},{9,8},{10,11... | collective-permute-start | bytes 786440 | tf_op jit(solution)/shard_map/ppermute | solution.py:387
  43.5 13.4 %collective-permute-start.8 = (f32[4,64,128]{2,1,0:T(8,128)S(1)}, f32[4,64,128]{2,1,0:T(8,128)S(1)}, u32[]{:S(2)}, u32[]{:S(2)}) collective-permute-start(f32[4,64,128]{2,1,0:T(8,128)S(1)} %pad_maximum_fusion.12), channel_id=1, source_target_pairs={{0,1},{1,2},{2,3},{3,4},{4,5},{5,6},{6,7},{7,0},{8,9},{9,10},{10,1... | collective-permute-start | bytes 393224 | tf_op jit(solution)/shard_map/ppermute | solution.py:301
  44.2 12.9 %collective-permute-start.9 = (f32[4,64,128]{2,1,0:T(8,128)S(1)}, f32[4,64,128]{2,1,0:T(8,128)S(1)}, u32[]{:S(2)}, u32[]{:S(2)}) collective-permute-start(f32[4,64,128]{2,1,0:T(8,128)S(1)} %pad_maximum_fusion.13), channel_id=1, source_target_pairs={{0,7},{1,0},{2,1},{3,2},{4,3},{5,4},{6,5},{7,6},{8,15},{9,8},{10,9... | collective-permute-start | bytes 393224 | tf_op jit(solution)/shard_map/ppermute | solution.py:301
  53.2 11.5 %collective-permute-start.6 = (f32[4,128,128]{2,1,0:T(8,128)S(1)}, f32[4,128,128]{2,1,0:T(8,128)S(1)}, u32[]{:S(2)}, u32[]{:S(2)}) collective-permute-start(f32[4,128,128]{2,1,0:T(8,128)S(1)} %pad_maximum_fusion.4), channel_id=1, source_target_pairs={{0,1},{1,2},{2,3},{3,4},{4,5},{5,6},{6,7},{7,0},{8,9},{9,10},{10,1... | collective-permute-start | bytes 786440 | tf_op jit(solution)/shard_map/ppermute | solution.py:301
  53.4 11.4 %collective-permute-start.7 = (f32[4,128,128]{2,1,0:T(8,128)S(1)}, f32[4,128,128]{2,1,0:T(8,128)S(1)}, u32[]{:S(2)}, u32[]{:S(2)}) collective-permute-start(f32[4,128,128]{2,1,0:T(8,128)S(1)} %pad_maximum_fusion.5), channel_id=1, source_target_pairs={{0,7},{1,0},{2,1},{3,2},{4,3},{5,4},{6,5},{7,6},{8,15},{9,8},{10,9... | collective-permute-start | bytes 786440 | tf_op jit(solution)/shard_map/ppermute | solution.py:301
  57.6 36.1 %collective-permute-start.10 = (f32[4,64,256]{2,1,0:T(8,128)S(1)}, f32[4,64,256]{2,1,0:T(8,128)S(1)}, u32[]{:S(2)}, u32[]{:S(2)}) collective-permute-start(f32[4,64,256]{2,1,0:T(8,128)S(1)} %get-tuple-element.46), channel_id=1, source_target_pairs={{0,8},{8,16},{16,24},{24,0},{1,9},{9,17},{17,25},{25,1},{2,10},{10... | collective-permute-start | bytes 786440 | tf_op jit(solution)/shard_map/ppermute | solution.py:301
  62.5 31.2 %collective-permute-start.11 = (f32[4,64,256]{2,1,0:T(8,128)S(1)}, f32[4,64,256]{2,1,0:T(8,128)S(1)}, u32[]{:S(2)}, u32[]{:S(2)}) collective-permute-start(f32[4,64,256]{2,1,0:T(8,128)S(1)} %get-tuple-element.47), channel_id=1, source_target_pairs={{0,24},{8,0},{16,8},{24,16},{1,25},{9,1},{17,9},{25,17},{2,26},{10... | collective-permute-start | bytes 786440 | tf_op jit(solution)/shard_map/ppermute | solution.py:301
  62.6 11.2 %collective-permute-start.13 = (f32[64,256]{1,0:T(8,128)S(1)}, f32[64,256]{1,0:T(8,128)S(1)}, u32[]{:S(2)}, u32[]{:S(2)}) collective-permute-start(f32[64,256]{1,0:T(8,128)S(1)} %get-tuple-element.67), channel_id=1, source_target_pairs={{0,8},{8,16},{16,24},{24,0},{1,9},{9,17},{17,25},{25,1},{2,10},{10... | collective-permute-start | bytes 196616 | tf_op jit(solution)/shard_map/ppermute | solution.py:387
  64.6 9.2 %collective-permute-start.14 = (f32[64,256]{1,0:T(8,128)S(1)}, f32[64,256]{1,0:T(8,128)S(1)}, u32[]{:S(2)}, u32[]{:S(2)}) collective-permute-start(f32[64,256]{1,0:T(8,128)S(1)} %get-tuple-element.69), channel_id=1, source_target_pairs={{0,16},{8,24},{16,0},{24,8},{1,17},{9,25},{17,1},{25,9},{2,18},{10... | collective-permute-start | bytes 196616 | tf_op jit(solution)/shard_map/ppermute | solution.py:387
  64.8 11.1 %collective-permute-start.15 = (f32[64,256]{1,0:T(8,128)S(1)}, f32[64,256]{1,0:T(8,128)S(1)}, u32[]{:S(2)}, u32[]{:S(2)}) collective-permute-start(f32[64,256]{1,0:T(8,128)S(1)} %get-tuple-element.68), channel_id=1, source_target_pairs={{0,24},{8,0},{16,8},{24,16},{1,25},{9,1},{17,9},{25,17},{2,26},{10... | collective-permute-start | bytes 196616 | tf_op jit(solution)/shard_map/ppermute | solution.py:387
  90.0 6.7 %collective-permute-start.22 = (f32[64,256]{1,0:T(8,128)S(1)}, f32[64,256]{1,0:T(8,128)S(1)}, u32[]{:S(2)}, u32[]{:S(2)}) collective-permute-start(f32[64,256]{1,0:T(8,128)S(1)} %bitcast.140), channel_id=1, source_target_pairs={{0,8},{8,16},{16,24},{24,0},{1,9},{9,17},{17,25},{25,1},{2,10},{10... | collective-permute-start | bytes 196616 | tf_op jit(solution)/shard_map/ppermute | solution.py:394
  90.4 6.5 %collective-permute-start.23 = (f32[64,256]{1,0:T(8,128)S(1)}, f32[64,256]{1,0:T(8,128)S(1)}, u32[]{:S(2)}, u32[]{:S(2)}) collective-permute-start(f32[64,256]{1,0:T(8,128)S(1)} %bitcast.141), channel_id=1, source_target_pairs={{0,16},{8,24},{16,0},{24,8},{1,17},{9,25},{17,1},{25,9},{2,18},{10... | collective-permute-start | bytes 196616 | tf_op jit(solution)/shard_map/ppermute | solution.py:394
  94.3 6.4 %collective-permute-start.26 = (f32[4,64,256]{2,1,0:T(8,128)S(1)}, f32[4,64,256]{2,1,0:T(8,128)S(1)}, u32[]{:S(2)}, u32[]{:S(2)}) collective-permute-start(f32[4,64,256]{2,1,0:T(8,128)S(1)} %get-tuple-element.30), channel_id=1, source_target_pairs={{0,24},{8,0},{16,8},{24,16},{1,25},{9,1},{17,9},{25,17},{2,26},{10... | collective-permute-start | bytes 786440 | tf_op jit(solution)/shard_map/ppermute | solution.py:301
  94.7 9.5 %collective-permute-start.27 = (f32[4,64,256]{2,1,0:T(8,128)S(1)}, f32[4,64,256]{2,1,0:T(8,128)S(1)}, u32[]{:S(2)}, u32[]{:S(2)}) collective-permute-start(f32[4,64,256]{2,1,0:T(8,128)S(1)} %get-tuple-element.31), channel_id=1, source_target_pairs={{0,8},{8,16},{16,24},{24,0},{1,9},{9,17},{17,25},{25,1},{2,10},{10... | collective-permute-start | bytes 786440 | tf_op jit(solution)/shard_map/ppermute | solution.py:301
  96.7 9.1 %collective-permute-start.28 = (f32[4,128,128]{2,1,0:T(8,128)S(1)}, f32[4,128,128]{2,1,0:T(8,128)S(1)}, u32[]{:S(2)}, u32[]{:S(2)}) collective-permute-start(f32[4,128,128]{2,1,0:T(8,128)S(1)} %pad_maximum_fusion.6), channel_id=1, source_target_pairs={{0,7},{1,0},{2,1},{3,2},{4,3},{5,4},{6,5},{7,6},{8,15},{9,8},{10,9... | collective-permute-start | bytes 786440 | tf_op jit(solution)/shard_map/ppermute | solution.py:301
  96.9 9.4 %collective-permute-start.29 = (f32[4,128,128]{2,1,0:T(8,128)S(1)}, f32[4,128,128]{2,1,0:T(8,128)S(1)}, u32[]{:S(2)}, u32[]{:S(2)}) collective-permute-start(f32[4,128,128]{2,1,0:T(8,128)S(1)} %pad_maximum_fusion.7), channel_id=1, source_target_pairs={{0,1},{1,2},{2,3},{3,4},{4,5},{5,6},{6,7},{7,0},{8,9},{9,10},{10,1... | collective-permute-start | bytes 786440 | tf_op jit(solution)/shard_map/ppermute | solution.py:301
  97.4 9.2 %collective-permute-start.25 = (f32[256,256]{1,0:T(8,128)S(1)}, f32[256,256]{1,0:T(8,128)S(1)}, u32[]{:S(2)}, u32[]{:S(2)}) collective-permute-start(f32[256,256]{1,0:T(8,128)S(1)} %bitcast.125), channel_id=1, source_target_pairs={{0,1},{1,0},{2,3},{3,2},{4,5},{5,4},{6,7},{7,6},{8,9},{9,8},{10,11... | collective-permute-start | bytes 786440 | tf_op jit(solution)/shard_map/ppermute | solution.py:394
  105.3 6.4 %collective-permute-start.31 = (f32[4,64,128]{2,1,0:T(8,128)}, f32[4,64,128]{2,1,0:T(8,128)S(1)}, u32[]{:S(2)}, u32[]{:S(2)}) collective-permute-start(f32[4,64,128]{2,1,0:T(8,128)} %pad_maximum_fusion.15), channel_id=1, source_target_pairs={{0,1},{1,2},{2,3},{3,4},{4,5},{5,6},{6,7},{7,0},{8,9},{9,10},{10,1... | collective-permute-start | bytes 393224 | tf_op jit(solution)/shard_map/ppermute | solution.py:301
  127.0 18.1 %collective-permute-start.38 = (f32[256,256]{1,0:T(8,128)S(1)}, f32[256,256]{1,0:T(8,128)S(1)}, u32[]{:S(2)}, u32[]{:S(2)}) collective-permute-start(f32[256,256]{1,0:T(8,128)S(1)} %dynamic-slice_bitcast_fusion), channel_id=1, source_target_pairs={{0,1},{1,0},{2,3},{3,2},{4,5},{5,4},{6,7},{7,6},{8,9},{9,8},{10,11... | collective-permute-start | bytes 786440 | tf_op jit(solution)/shard_map/ppermute | solution.py:387
  127.4 12.4 %collective-permute-start.34 = (f32[4,64,128]{2,1,0:T(8,128)S(1)}, f32[4,64,128]{2,1,0:T(8,128)S(1)}, u32[]{:S(2)}, u32[]{:S(2)}) collective-permute-start(f32[4,64,128]{2,1,0:T(8,128)S(1)} %pad_maximum_fusion.16), channel_id=1, source_target_pairs={{0,1},{1,2},{2,3},{3,4},{4,5},{5,6},{6,7},{7,0},{8,9},{9,10},{10,1... | collective-permute-start | bytes 393224 | tf_op jit(solution)/shard_map/ppermute | solution.py:301
  128.0 11.9 %collective-permute-start.35 = (f32[4,64,128]{2,1,0:T(8,128)S(1)}, f32[4,64,128]{2,1,0:T(8,128)S(1)}, u32[]{:S(2)}, u32[]{:S(2)}) collective-permute-start(f32[4,64,128]{2,1,0:T(8,128)S(1)} %pad_maximum_fusion.17), channel_id=1, source_target_pairs={{0,7},{1,0},{2,1},{3,2},{4,3},{5,4},{6,5},{7,6},{8,15},{9,8},{10,9... | collective-permute-start | bytes 393224 | tf_op jit(solution)/shard_map/ppermute | solution.py:301
  136.0 11.3 %collective-permute-start.32 = (f32[4,128,128]{2,1,0:T(8,128)S(1)}, f32[4,128,128]{2,1,0:T(8,128)S(1)}, u32[]{:S(2)}, u32[]{:S(2)}) collective-permute-start(f32[4,128,128]{2,1,0:T(8,128)S(1)} %pad_maximum_fusion.8), channel_id=1, source_target_pairs={{0,1},{1,2},{2,3},{3,4},{4,5},{5,6},{6,7},{7,0},{8,9},{9,10},{10,1... | collective-permute-start | bytes 786440 | tf_op jit(solution)/shard_map/ppermute | solution.py:301
  136.2 12.7 %collective-permute-start.33 = (f32[4,128,128]{2,1,0:T(8,128)S(1)}, f32[4,128,128]{2,1,0:T(8,128)S(1)}, u32[]{:S(2)}, u32[]{:S(2)}) collective-permute-start(f32[4,128,128]{2,1,0:T(8,128)S(1)} %pad_maximum_fusion.9), channel_id=1, source_target_pairs={{0,7},{1,0},{2,1},{3,2},{4,3},{5,4},{6,5},{7,6},{8,15},{9,8},{10,9... | collective-permute-start | bytes 786440 | tf_op jit(solution)/shard_map/ppermute | solution.py:301
  140.5 39.7 %collective-permute-start.36 = (f32[4,64,256]{2,1,0:T(8,128)S(1)}, f32[4,64,256]{2,1,0:T(8,128)S(1)}, u32[]{:S(2)}, u32[]{:S(2)}) collective-permute-start(f32[4,64,256]{2,1,0:T(8,128)S(1)} %get-tuple-element.38), channel_id=1, source_target_pairs={{0,8},{8,16},{16,24},{24,0},{1,9},{9,17},{17,25},{25,1},{2,10},{10... | collective-permute-start | bytes 786440 | tf_op jit(solution)/shard_map/ppermute | solution.py:301
  145.1 35.1 %collective-permute-start.37 = (f32[4,64,256]{2,1,0:T(8,128)S(1)}, f32[4,64,256]{2,1,0:T(8,128)S(1)}, u32[]{:S(2)}, u32[]{:S(2)}) collective-permute-start(f32[4,64,256]{2,1,0:T(8,128)S(1)} %get-tuple-element.39), channel_id=1, source_target_pairs={{0,24},{8,0},{16,8},{24,16},{1,25},{9,1},{17,9},{25,17},{2,26},{10... | collective-permute-start | bytes 786440 | tf_op jit(solution)/shard_map/ppermute | solution.py:301
  145.2 11.9 %collective-permute-start.39 = (f32[64,256]{1,0:T(8,128)S(1)}, f32[64,256]{1,0:T(8,128)S(1)}, u32[]{:S(2)}, u32[]{:S(2)}) collective-permute-start(f32[64,256]{1,0:T(8,128)S(1)} %get-tuple-element.54), channel_id=1, source_target_pairs={{0,8},{8,16},{16,24},{24,0},{1,9},{9,17},{17,25},{25,1},{2,10},{10... | collective-permute-start | bytes 196616 | tf_op jit(solution)/shard_map/ppermute | solution.py:387
  147.3 9.8 %collective-permute-start.40 = (f32[64,256]{1,0:T(8,128)S(1)}, f32[64,256]{1,0:T(8,128)S(1)}, u32[]{:S(2)}, u32[]{:S(2)}) collective-permute-start(f32[64,256]{1,0:T(8,128)S(1)} %get-tuple-element.56), channel_id=1, source_target_pairs={{0,16},{8,24},{16,0},{24,8},{1,17},{9,25},{17,1},{25,9},{2,18},{10... | collective-permute-start | bytes 196616 | tf_op jit(solution)/shard_map/ppermute | solution.py:387
  148.9 11.1 %collective-permute-start.41 = (f32[64,256]{1,0:T(8,128)S(1)}, f32[64,256]{1,0:T(8,128)S(1)}, u32[]{:S(2)}, u32[]{:S(2)}) collective-permute-start(f32[64,256]{1,0:T(8,128)S(1)} %get-tuple-element.55), channel_id=1, source_target_pairs={{0,24},{8,0},{16,8},{24,16},{1,25},{9,1},{17,9},{25,17},{2,26},{10... | collective-permute-start | bytes 196616 | tf_op jit(solution)/shard_map/ppermute | solution.py:387
  (26 other events, 126.1 us)
